TPU v7x, 32 devices: a whole 2x2x4 slice. The times are simulated.
32 devices in a mesh: row: 4 (over x, core), col: 8 (over z, y).
Axes of the slice: x: 2, y: 2, z: 4, core: 2. Of those that a mesh axis runs over, the one named last changes fastest.
Arguments:
- tensor: float32 [1024, 32, 1024], P(None, 'row', 'col'), may hold values from -60 to 60, as said below
- factor_two: float32 [32, 32], P('row'), may hold values from -1 to 1
- factor_three: float32 [32, 32], P('col'), may hold values from -1 to 1
- factor_four: float32 [32, 16], replicated, may hold values from -1 to 1
- factor_init: float32 [1024, 64], replicated, may hold values from -6 to 6
Outputs:
- factor_new: float32 [1024, 64], replicated
- core: float32 [64, 32, 32, 16], P(None, 'row', 'col')
Inputs may be any that keep to these rules, and one draw needn't show every extreme that they name: `tensor`: scales vary from slab to slab.
All inputs are finite; a program needn't handle non-finite values.
Results may differ from a plain program's by a relative error of at most 0.00013.
Values sent between devices are 32-bit elements; how exact they have to be, the bound alone decides.
A program may use at most 128 MiB of HBM per device.

v0:
```python
import jax
import jax.numpy as jnp
from jax import lax
from jax.sharding import PartitionSpec as P


def shards(tensor, factor_two, factor_three, factor_four, factor_init):
    highest = lax.Precision.HIGHEST
    first_len = tensor.shape[0]
    local_two = tensor.shape[1]
    fourth_len = factor_four.shape[0]
    local_three = tensor.shape[2] // fourth_len
    rank_one = factor_init.shape[1]
    data = tensor.reshape(first_len, local_two, local_three, fourth_len)
    fourth = jnp.einsum("abcd,de->abce", data, factor_four, precision=highest)
    whole_two = lax.all_gather(factor_two, "row", axis=0, tiled=True)
    spread_two = lax.all_to_all(fourth, "row", split_axis=0, concat_axis=1, tiled=True)
    projected_two = jnp.einsum("abce,bg->agce", spread_two, whole_two, precision=highest)
    partial_two = lax.all_to_all(projected_two, "row", split_axis=1, concat_axis=0, tiled=True)
    whole_three = lax.all_gather(factor_three, "col", axis=0, tiled=True)
    spread_three = lax.all_to_all(partial_two, "col", split_axis=0, concat_axis=2, tiled=True)
    projected_three = jnp.einsum("agce,cf->agfe", spread_three, whole_three, precision=highest)
    block = lax.all_to_all(projected_three, "col", split_axis=2, concat_axis=0, tiled=True)
    columns = block.reshape(first_len, -1)
    basis = factor_init
    local_gram = jnp.dot(columns, columns.T, precision=highest, preferred_element_type=jnp.float32)
    gram = lax.psum(local_gram, ("row", "col"))
    image = jnp.dot(gram, basis, precision=highest, preferred_element_type=jnp.float32)
    square = jnp.dot(image.T, image, precision=highest, preferred_element_type=jnp.float32)
    lower = jnp.linalg.cholesky(square)
    basis = jax.scipy.linalg.solve_triangular(lower, image.T, lower=True).T
    core = jnp.dot(basis.T, columns, precision=highest, preferred_element_type=jnp.float32)
    return (basis, core.reshape(rank_one, block.shape[1], block.shape[2], block.shape[3]))


def solution(mesh):
    in_specs = (P(None, "row", "col"), P("row", None), P("col", None), P(), P())
    out_specs = (P(), P(None, "row", "col", None))
    return jax.shard_map(shards, mesh=mesh, in_specs=in_specs, out_specs=out_specs, check_vma=False)
```

profile of v0, /device:TPU:0, one launch (start us, length us, event | category | flops | bytes accessed | tf_op | source)
XLA Modules:
  0.0 512.5 jit_solution(1816454857235836736)
XLA Ops:
  7.2 0.0 copy-start
  7.2 0.0 copy-start.4
  7.2 5.5 %copy.18 = f32[1024,8,128]{0,2,1:T(8,128)} copy(f32[1024,8,128]{2,1,0:T(8,128)} %param.5) | data formatting | bytes 8388608 | tf_op args[0]
  12.6 0.0 copy-done.4
  12.6 4.2 fusion.12
  16.8 12.2 %copy.19 = f32[1024,8,4,16]{3,2,1,0:T(4,128)} copy(f32[1024,8,4,16]{0,3,2,1:T(8,128)S(1)} %fusion.12) | data formatting | bytes 4194304 | tf_op jit(solution)/shard_map/abcd,de->abce/dot_general | solution.py:15
  29.0 15.5 %reshape.31 = f32[4,1,131072]{2,1,0:T(1,128)} reshape(f32[1024,8,4,16]{3,2,1,0:T(4,128)} %copy.19) | data formatting | bytes 4194304
  44.5 4.4 all-to-all-start
  48.9 26.7 %all_gather.6 = f32[32,32]{1,0:T(8,128)S(1)} all-gather(f32[8,32]{1,0:T(8,128)S(1)} %copy-done.5), channel_id=1, replica_groups=mesh['row'=4,'col'=8] {'row'}, dimensions={0}, use_global_device_ids=true | all-gather | bytes 5120 | tf_op jit(solution)/shard_map/all_gather | solution.py:16
  75.5 0.0 all-to-all-done
  75.5 1.4 copy-done.2
  76.9 0.5 broadcast.53
  77.4 7.7 %reduce.6 = f32[4,131072]{1,0:T(4,128)S(1)} reduce(f32[4,1,131072]{2,1,0:T(1,128)} %copy-done.2, f32[]{:T(128)} %broadcast.53), dimensions={1}, to_apply=%all_to_all.50.reduce_sub_computation | reduce | bytes 4194308 | tf_op jit(solution)/shard_map/all_to_all | solution.py:17
  85.1 17.9 %reshape.32 = f32[1024,8,4,16]{3,2,1,0:T(4,128)} reshape(f32[4,131072]{1,0:T(4,128)S(1)} %reduce.6) | data formatting | bytes 4194304
  103.0 12.2 %copy.20 = f32[4,256,8,4,16]{1,2,0,4,3:T(8,128)S(1)} copy(f32[4,256,8,4,16]{4,3,2,1,0:T(4,128)} %bitcast.72) | data formatting | bytes 4194304 | tf_op jit(solution)/shard_map/all_to_all | solution.py:17
  115.3 1.9 fusion.2
  117.2 1.2 copy.21
  118.4 28.1 %all_to_all.69 = f32[256,32,4,16]{0,3,2,1:T(8,128)S(1)} all-to-all(f32[256,32,4,16]{0,3,2,1:T(8,128)S(1)} %copy.21), channel_id=1, replica_groups=mesh['row'=4,'col'=8] {'row'}, dimensions={1} | all-to-all | bytes 4194304 | tf_op jit(solution)/shard_map/all_to_all | solution.py:19
  146.6 12.1 %copy.37 = f32[256,4,8,4,16]{4,3,2,0,1:T(4,128)} copy(f32[256,4,8,4,16]{0,4,3,2,1:T(8,128)S(1)} %bitcast.78) | data formatting | bytes 4194304 | tf_op jit(solution)/shard_map/all_to_all | solution.py:19
  158.6 15.4 %reshape.33 = f32[8,1,65536]{2,1,0:T(1,128)} reshape(f32[1024,8,4,16]{3,2,1,0:T(4,128)} %bitcast.73) | data formatting | bytes 4194304
  174.0 6.8 %all-to-all-start.2 = ((f32[8,1,65536]{2,1,0:T(1,128)}), f32[8,1,65536]{2,1,0:T(1,128)}, u32[]{:S(2)}, u32[]{:S(2)}) async-start(f32[8,1,65536]{2,1,0:T(1,128)} %reshape.33), calls=%async_computation.2 | async-start | bytes 4194304 | tf_op jit(solution)/shard_map/all_to_all | solution.py:21
  180.8 0.0 all-reduce.2.cloned.1.call-start
  180.9 66.5 %all-gather = f32[8,4,32]{2,1,0:T(4,128)S(1)} all-gather(f32[1,4,32]{2,1,0:T(4,128)S(1)} %bitcast.85), channel_id=1, replica_groups=mesh['row'=4,'col'=8] {'col'}, dimensions={0}, use_global_device_ids=true | all-gather | bytes 4608 | tf_op jit(solution)/shard_map/all_gather | solution.py:20
  247.3 0.0 all-to-all-done.2
  247.3 7.2 %reduce.7 = f32[8,65536]{1,0:T(8,128)S(1)} reduce(f32[8,1,65536]{2,1,0:T(1,128)} %all-to-all-done.2, f32[]{:T(128)} %broadcast.53), dimensions={1}, to_apply=%all_to_all.58.reduce_sub_computation | reduce | bytes 4194308 | tf_op jit(solution)/shard_map/all_to_all | solution.py:21
  254.6 17.3 %reshape.34 = f32[1024,8,4,16]{3,2,1,0:T(4,128)} reshape(f32[8,65536]{1,0:T(8,128)S(1)} %reduce.7) | data formatting | bytes 4194304
  271.9 9.8 %copy.35 = f32[8,128,8,4,16]{1,0,4,3,2:T(8,128)S(1)} copy(f32[8,128,8,4,16]{4,3,2,1,0:T(4,128)} %bitcast.74) | data formatting | bytes 4194304 | tf_op jit(solution)/shard_map/all_to_all | solution.py:21
  281.7 1.4 copy.25
  283.1 1.9 convolution_bitcast_fusion
  285.0 1.2 copy.27
  286.2 46.2 %all_to_all.70 = f32[128,8,32,16]{0,3,1,2:T(8,128)S(1)} all-to-all(f32[128,8,32,16]{0,3,1,2:T(8,128)S(1)} %copy.27), channel_id=1, replica_groups=mesh['row'=4,'col'=8] {'col'}, dimensions={2} | all-to-all | bytes 4194304 | tf_op jit(solution)/shard_map/all_to_all | solution.py:23
  332.5 1.2 copy.28
  333.7 8.9 %fusion.14 = f32[1024,1024]{1,0:T(8,128)} fusion(f32[64,8,8,128]{3,2,1,0:T(8,128)S(1)} %bitcast.75), kind=kOutput, calls=%fused_computation.20 | convolution fusion | flops 6442450944 | bytes 6291456 | tf_op jit(solution)/shard_map/dot_general | solution.py:26
  342.6 0.0 all-reduce.2.cloned.1.call-update
  342.7 1.9 copy.41
  344.5 138.8 %all-reduce.2.cloned.1.call-done = f32[1024,1024]{1,0:T(8,128)} async-done(((f32[1024,1024]{1,0:T(8,128)}), f32[1024,1024]{1,0:T(8,128)}) %all-reduce.2.cloned.1.call-update) | async-done | bytes 4194320 | tf_op jit(solution)/shard_map/psum | solution.py:27
  483.4 6.3 %fusion.15 = f32[1024,64]{0,1:T(8,128)S(1)} fusion(f32[1024,1024]{1,0:T(8,128)} %all-reduce.2.cloned.1.call-done, f32[1024,64]{0,1:T(8,128)S(1)} %copy-done), kind=kOutput, calls=%fused_computation.21 | convolution fusion | flops 805306368 | bytes 4718592 | tf_op jit(solution)/shard_map/dot_general | solution.py:28
  489.7 0.4 fusion.16
  490.1 0.1 copy.29
  490.2 5.8 %cholesky.16 = f32[64,64]{1,0:T(8,128)S(1)} custom-call(f32[64,64]{1,0:T(8,128)S(1)} %fusion.10), custom_call_target="Cholesky" | custom-call | tf_op jit(solution)/shard_map/jit(cholesky)/cholesky | solution.py:30
  496.0 0.6 compare_reduce_fusion
  496.7 0.7 fusion.7
  497.3 4.9 custom-call.7
  502.2 0.4 fusion.8
  502.7 0.0 copy-start.3
  502.7 0.0 copy-done.1
  502.7 2.5 fusion.5
  505.2 0.0 copy-done.3
  (9 shorter events, 0.1 us)
Async XLA Ops:
  7.2 476.2 %copy-start = (f32[1024,64]{0,1:T(8,128)S(1)}, f32[1024,64]{0,1:T(8,128)}, u32[]{:S(2)}) copy-start(f32[1024,64]{0,1:T(8,128)} %param.9) | copy-start | bytes 786436
  7.2 5.5 %copy-start.4 = (f32[32,16]{0,1:T(8,128)S(1)}, f32[32,16]{0,1:T(8,128)}, u32[]{:S(2)}) copy-start(f32[32,16]{0,1:T(8,128)} %param.8) | copy-start | bytes 6148
  44.5 4.4 copy-start.5
  44.5 31.1 %all-to-all-start = ((f32[4,1,131072]{2,1,0:T(1,128)}), f32[4,1,131072]{2,1,0:T(1,128)S(1)}, u32[]{:S(2)}, u32[]{:S(2)}) async-start(f32[4,1,131072]{2,1,0:T(1,128)} %reshape.31), calls=%async_computation | async-start | bytes 4194304 | tf_op jit(solution)/shard_map/all_to_all | solution.py:17
  75.5 1.4 copy-start.2
  174.0 6.8 %copy-start.6 = (f32[4,32]{1,0:T(4,128)S(1)}, f32[4,32]{1,0:T(4,128)}, u32[]{:S(2)}) copy-start(f32[4,32]{1,0:T(4,128)} %param.7) | copy-start | bytes 1540
  174.0 73.3 %all-to-all-start.2 = ((f32[8,1,65536]{2,1,0:T(1,128)}), f32[8,1,65536]{2,1,0:T(1,128)}, u32[]{:S(2)}, u32[]{:S(2)}) async-start(f32[8,1,65536]{2,1,0:T(1,128)} %reshape.33), calls=%async_computation.2 | async-start | bytes 4194304 | tf_op jit(solution)/shard_map/all_to_all | solution.py:21
  180.8 302.5 %all-reduce.2.cloned.1.call-start = ((), (), s32[]{:S(2)}) async-start(), calls=%async_computation.4 | async-start | bytes 8388608 | tf_op jit(solution)/shard_map/psum | solution.py:27
  344.5 158.2 %copy-start.1 = (f32[64,8,8,128]{3,1,2,0:T(8,128)S(1)}, f32[64,8,8,128]{3,1,2,0:T(8,128)}, u32[]{:S(2)}) copy-start(f32[64,8,8,128]{3,1,2,0:T(8,128)} %copy.41) | copy-start | bytes 6291460
  502.7 2.5 copy-start.3
Sparse Core Ops, SparseCore 0:
  342.8 140.5 all-reduce.1
where the time goes:
time: 518 us; the launch traced here: 512 us
  blocking collectives  168 us (32%)
  waiting for transfers between devices  139 us (27%)
  local copies, waits for them, and re-layouts  127 us (25%)
  other arithmetic  27 us (5%)
  matrix products  26.5 us (5%)
  between operations  14.6 us (3%)
  starting transfers between devices  11.2 us (2%)
    psum x1, waiting for transfers between devices, shards(): gram = lax.psum(local_gram, ('row', 'col'))  139 us
    unnamed x20, local copies, waits for them, and re-layouts  74.8 us
    all_gather x1, blocking collectives, shards(): whole_three = lax.all_gather(factor_three, 'col', axis=0, tiled=True)  66.5 us
    all_to_all x1, blocking collectives, shards(): lax.all_to_all(projected_three, 'col', split_axis=2, concat_axis=0, tiled...  46.2 us
    all_to_all x1, blocking collectives, shards(): lax.all_to_all(projected_two, 'row', split_axis=1, concat_axis=0, tiled=T...  28.1 us
    all_gather x1, blocking collectives, shards(): whole_two = lax.all_gather(factor_two, 'row', axis=0, tiled=True)  26.7 us
    all_to_all x2, local copies, waits for them, and re-layouts, shards(): lax.all_to_all(fourth, 'row', split_axis=0, concat_axis=1, tiled=True)  12.7 us
    dot_general x1, local copies, waits for them, and re-layouts, shards(): fourth = jnp.einsum('abcd,de->abce', data, factor_four, precision=highest)  12.2 us
  transfers between devices with their start and end apart: 3, of which 1 were waited for; matrix products, arithmetic and copies ran while one was open for 0% of the time, Pallas kernels for 0%

commit v1 on v0

--- a/solution.py
+++ b/solution.py
@@ -16,7 +16,20 @@
     whole_two = lax.all_gather(factor_two, "row", axis=0, tiled=True)
     spread_two = lax.all_to_all(fourth, "row", split_axis=0, concat_axis=1, tiled=True)
     projected_two = jnp.einsum("abce,bg->agce", spread_two, whole_two, precision=highest)
-    partial_two = lax.all_to_all(projected_two, "row", split_axis=1, concat_axis=0, tiled=True)
+    z1, x_next = (lax.axis_size("row"), lax.axis_index("row"))
+    newest = projected_two.shape[1] // z1
+    b_next = list(projected_two.shape)
+    b_next[1] = newest
+    block_last = b_next[0]
+    b_next[0] = block_last * z1
+    partial_two = jnp.zeros(b_next, projected_two.dtype)
+    for b in tuple(range(z1)):
+        kept_arr = lax.dynamic_slice_in_dim(projected_two, (x_next ^ b) * newest, newest, axis=1)
+        if b:
+            kept_arr = lax.ppermute(kept_arr, "row", tuple(((rr, rr ^ b) for rr in range(z1))))
+        partial_two = lax.dynamic_update_slice_in_dim(
+            partial_two, kept_arr, (x_next ^ b) * block_last, axis=0
+        )
     whole_three = lax.all_gather(factor_three, "col", axis=0, tiled=True)
     spread_three = lax.all_to_all(partial_two, "col", split_axis=0, concat_axis=2, tiled=True)
     projected_three = jnp.einsum("agce,cf->agfe", spread_three, whole_three, precision=highest)

time: 518 us -> 520 us (level)
  local copies, waits for them, and re-layouts: 127 us -> 154 us
  blocking collectives: 168 us -> 141 us
    all_to_all x1 -> x0, blocking collectives: 28.1 us -> none  [shards(): lax.all_to_all(projected_two, 'row', split_axis=1, concat_axis=0, tiled=T...]
    dynamic_update_slice x0 -> x4, local copies, waits for them, and re-layouts: none -> 16.2 us  [shards(): lax.dynamic_update_slice_in_dim(partial_two, kept_arr, (x_next ^ b) * blo...]
    ppermute x0 -> x3, local copies, waits for them, and re-layouts: none -> 13.3 us  [shards(): lax.ppermute(kept_arr, 'row', tuple(((rr, rr ^ b) for rr in range(z1))))]
    all_to_all x1 -> x0, local copies, waits for them, and re-layouts: 12.1 us -> none  [shards(): lax.all_to_all(projected_two, 'row', split_axis=1, concat_axis=0, tiled=T...]
    broadcast_in_dim x0 -> x1, local copies, waits for them, and re-layouts: none -> 6.34 us  [shards(): partial_two = jnp.zeros(b_next, projected_two.dtype)]
    unnamed x20 -> x24, local copies, waits for them, and re-layouts: 74.8 us -> 74.8 us
  transfers between devices with their start and end apart: 3 -> 6, of which waited for: 1 -> 1; matrix products, arithmetic and copies ran while one was open for 0% -> 6% of each run, Pallas kernels for 0% -> 0%
where the time goes in v1:
time: 520 us; the launch traced here: 515 us
  local copies, waits for them, and re-layouts  154 us (30%)
  blocking collectives  141 us (27%)
  waiting for transfers between devices  139 us (27%)
  other arithmetic  27 us (5%)
  matrix products  26.5 us (5%)
  between operations  14.6 us (3%)
  starting transfers between devices  13.1 us (3%)
    psum x1, waiting for transfers between devices, shards(): gram = lax.psum(local_gram, ('row', 'col'))  139 us
    unnamed x24, local copies, waits for them, and re-layouts  74.8 us
    all_gather x1, blocking collectives, shards(): whole_three = lax.all_gather(factor_three, 'col', axis=0, tiled=True)  67.6 us
    all_to_all x1, blocking collectives, shards(): lax.all_to_all(projected_three, 'col', split_axis=2, concat_axis=0, tiled...  46.3 us
    all_gather x1, blocking collectives, shards(): whole_two = lax.all_gather(factor_two, 'row', axis=0, tiled=True)  26.7 us
    dynamic_update_slice x4, local copies, waits for them, and re-layouts, shards(): lax.dynamic_update_slice_in_dim(partial_two, kept_arr, (x_next ^ b) * blo...  16.2 us
    ppermute x3, local copies, waits for them, and re-layouts, shards(): lax.ppermute(kept_arr, 'row', tuple(((rr, rr ^ b) for rr in range(z1))))  13.3 us
    all_to_all x2, local copies, waits for them, and re-layouts, shards(): lax.all_to_all(fourth, 'row', split_axis=0, concat_axis=1, tiled=True)  12.7 us
  transfers between devices with their start and end apart: 6, of which 1 were waited for; matrix products, arithmetic and copies ran while one was open for 6% of the time, Pallas kernels for 0%

profile of v1, /device:TPU:0, one launch (start us, length us, event | category | flops | bytes accessed | tf_op | source)
XLA Modules:
  0.0 514.6 jit_solution(8935516204427921779)
XLA Ops:
  7.2 5.5 %copy.21 = f32[1024,8,128]{0,2,1:T(8,128)} copy(f32[1024,8,128]{2,1,0:T(8,128)} %param.5) | data formatting | bytes 8388608 | tf_op args[0]
  12.7 4.2 fusion.9
  16.8 12.1 %copy.22 = f32[1024,8,4,16]{3,2,1,0:T(4,128)} copy(f32[1024,8,4,16]{0,3,2,1:T(8,128)S(1)} %fusion.9) | data formatting | bytes 4194304 | tf_op jit(solution)/shard_map/abcd,de->abce/dot_general | solution.py:15
  28.9 15.5 %reshape.31 = f32[4,1,131072]{2,1,0:T(1,128)} reshape(f32[1024,8,4,16]{3,2,1,0:T(4,128)} %copy.22) | data formatting | bytes 4194304
  44.4 4.4 all-to-all-start
  48.8 26.7 %all_gather.6 = f32[32,32]{1,0:T(8,128)S(1)} all-gather(f32[8,32]{1,0:T(8,128)S(1)} %copy-done.7), channel_id=1, replica_groups=mesh['row'=4,'col'=8] {'row'}, dimensions={0}, use_global_device_ids=true | all-gather | bytes 5120 | tf_op jit(solution)/shard_map/all_gather | solution.py:16
  75.5 1.3 copy-done.4
  76.8 0.5 broadcast.53
  77.3 7.7 %reduce.6 = f32[4,131072]{1,0:T(4,128)S(1)} reduce(f32[4,1,131072]{2,1,0:T(1,128)} %copy-done.4, f32[]{:T(128)} %broadcast.53), dimensions={1}, to_apply=%all_to_all.37.reduce_sub_computation | reduce | bytes 4194308 | tf_op jit(solution)/shard_map/all_to_all | solution.py:17
  85.0 18.0 %reshape.32 = f32[1024,8,4,16]{3,2,1,0:T(4,128)} reshape(f32[4,131072]{1,0:T(4,128)S(1)} %reduce.6) | data formatting | bytes 4194304
  103.0 12.2 %copy.23 = f32[4,256,8,4,16]{1,2,0,4,3:T(8,128)S(1)} copy(f32[4,256,8,4,16]{4,3,2,1,0:T(4,128)} %bitcast.71) | data formatting | bytes 4194304 | tf_op jit(solution)/shard_map/all_to_all | solution.py:17
  115.2 1.9 fusion
  117.2 0.2 dynamic-slice_bitcast_fusion
  117.4 0.4 collective-permute-start
  117.8 0.4 collective-permute-start.1
  118.2 4.4 copy.24
  122.6 1.1 collective-permute-start.2
  123.7 6.3 %broadcast_in_dim.5 = f32[1024,8,4,16]{3,2,1,0:T(4,128)} broadcast(f32[]{:T(128)} %constant.52.clone.1), dimensions={} | broadcast | bytes 2097156 | tf_op jit(solution)/shard_map/broadcast_in_dim | solution.py:25
  130.1 2.9 constant_dynamic-update-slice_fusion.3
  133.0 4.4 copy.25
  137.3 4.4 copy.26
  141.7 5.3 %constant_dynamic-update-slice_fusion.2 = f32[1024,8,4,16]{3,2,1,0:T(4,128)} fusion(f32[1024,8,4,16]{3,2,1,0:T(4,128)} %constant_dynamic-update-slice_fusion.3, f32[256,8,4,16]{3,2,1,0:T(4,128)} %copy.25, s32[]{:T(128)S(6)} %select_n.31), kind=kLoop, calls=%fused_computation.24 | loop fusion | bytes 8388612 | tf_op jit(solution)/shard_map/dynamic_update_slice | solution.py:30
  147.0 2.9 constant_dynamic-update-slice_fusion.1
  149.9 4.5 copy.27
  154.5 5.1 constant_dynamic-update-slice_fusion
  159.6 15.4 %reshape.33 = f32[8,1,65536]{2,1,0:T(1,128)} reshape(f32[1024,8,4,16]{3,2,1,0:T(4,128)} %constant_dynamic-update-slice_fusion) | data formatting | bytes 4194304
  174.9 6.8 %all-to-all-start.1 = ((f32[8,1,65536]{2,1,0:T(1,128)}), f32[8,1,65536]{2,1,0:T(1,128)}, u32[]{:S(2)}, u32[]{:S(2)}) async-start(f32[8,1,65536]{2,1,0:T(1,128)} %reshape.33), calls=%async_computation.1 | async-start | bytes 4194304 | tf_op jit(solution)/shard_map/all_to_all | solution.py:34
  181.8 67.6 %all-gather = f32[8,4,32]{2,1,0:T(4,128)S(1)} all-gather(f32[1,4,32]{2,1,0:T(4,128)S(1)} %bitcast.82), channel_id=1, replica_groups=mesh['row'=4,'col'=8] {'col'}, dimensions={0}, use_global_device_ids=true | all-gather | bytes 4608 | tf_op jit(solution)/shard_map/all_gather | solution.py:33
  249.4 7.2 %reduce.7 = f32[8,65536]{1,0:T(8,128)S(1)} reduce(f32[8,1,65536]{2,1,0:T(1,128)} %all-to-all-done.1, f32[]{:T(128)} %broadcast.53), dimensions={1}, to_apply=%all_to_all.41.reduce_sub_computation | reduce | bytes 4194308 | tf_op jit(solution)/shard_map/all_to_all | solution.py:34
  256.6 17.3 %reshape.34 = f32[1024,8,4,16]{3,2,1,0:T(4,128)} reshape(f32[8,65536]{1,0:T(8,128)S(1)} %reduce.7) | data formatting | bytes 4194304
  273.9 9.8 %copy.38 = f32[8,128,8,4,16]{1,0,4,3,2:T(8,128)S(1)} copy(f32[8,128,8,4,16]{4,3,2,1,0:T(4,128)} %bitcast.72) | data formatting | bytes 4194304 | tf_op jit(solution)/shard_map/all_to_all | solution.py:34
  283.7 1.4 copy.29
  285.1 1.9 convolution_bitcast_fusion
  287.1 1.2 copy.31
  288.3 46.3 %all_to_all.51 = f32[128,8,32,16]{0,3,1,2:T(8,128)S(1)} all-to-all(f32[128,8,32,16]{0,3,1,2:T(8,128)S(1)} %copy.31), channel_id=1, replica_groups=mesh['row'=4,'col'=8] {'col'}, dimensions={2} | all-to-all | bytes 4194304 | tf_op jit(solution)/shard_map/all_to_all | solution.py:36
  334.5 1.2 copy.32
  335.8 8.9 %fusion.11 = f32[1024,1024]{1,0:T(8,128)} fusion(f32[64,8,8,128]{3,2,1,0:T(8,128)S(1)} %bitcast.73), kind=kOutput, calls=%fused_computation.27 | convolution fusion | flops 6442450944 | bytes 6291456 | tf_op jit(solution)/shard_map/dot_general | solution.py:39
  344.7 1.8 copy.43
  346.6 138.9 %all-reduce.2.cloned.1.call-done = f32[1024,1024]{1,0:T(8,128)} async-done(((f32[1024,1024]{1,0:T(8,128)}), f32[1024,1024]{1,0:T(8,128)}) %all-reduce.2.cloned.1.call-update) | async-done | bytes 4194320 | tf_op jit(solution)/shard_map/psum | solution.py:40
  485.5 6.3 %fusion.12 = f32[1024,64]{0,1:T(8,128)S(1)} fusion(f32[1024,1024]{1,0:T(8,128)} %all-reduce.2.cloned.1.call-done, f32[1024,64]{0,1:T(8,128)S(1)} %copy-done), kind=kOutput, calls=%fused_computation.28 | convolution fusion | flops 805306368 | bytes 4718592 | tf_op jit(solution)/shard_map/dot_general | solution.py:41
  491.9 0.4 fusion.13
  492.2 0.1 copy.33
  492.3 5.8 %cholesky.16 = f32[64,64]{1,0:T(8,128)S(1)} custom-call(f32[64,64]{1,0:T(8,128)S(1)} %fusion.7), custom_call_target="Cholesky" | custom-call | tf_op jit(solution)/shard_map/jit(cholesky)/cholesky | solution.py:43
  498.2 0.6 compare_reduce_fusion
  498.8 0.7 fusion.4
  499.5 4.9 custom-call.7
  504.4 0.4 fusion.5
  504.9 2.5 fusion.2
  (26 shorter events, 0.1 us)
Async XLA Ops:
  7.2 478.4 %copy-start = (f32[1024,64]{0,1:T(8,128)S(1)}, f32[1024,64]{0,1:T(8,128)}, u32[]{:S(2)}) copy-start(f32[1024,64]{0,1:T(8,128)} %param.9) | copy-start | bytes 786436
  7.2 5.5 %copy-start.6 = (f32[32,16]{0,1:T(8,128)S(1)}, f32[32,16]{0,1:T(8,128)}, u32[]{:S(2)}) copy-start(f32[32,16]{0,1:T(8,128)} %param.8) | copy-start | bytes 6148
  44.4 4.4 copy-start.7
  44.4 31.1 %all-to-all-start = ((f32[4,1,131072]{2,1,0:T(1,128)}), f32[4,1,131072]{2,1,0:T(1,128)S(1)}, u32[]{:S(2)}, u32[]{:S(2)}) async-start(f32[4,1,131072]{2,1,0:T(1,128)} %reshape.31), calls=%async_computation | async-start | bytes 4194304 | tf_op jit(solution)/shard_map/all_to_all | solution.py:17
  75.5 1.3 copy-start.4
  117.4 15.5 %collective-permute-start = (f32[256,8,4,16]{0,1,3,2:T(8,128)S(1)}, f32[256,8,4,16]{0,1,3,2:T(8,128)S(1)}, u32[]{:S(2)}, u32[]{:S(2)}) collective-permute-start(f32[256,8,4,16]{0,1,3,2:T(8,128)S(1)} %get-tuple-element.4), channel_id=1, source_target_pairs={{0,8},{8,0},{16,24},{24,16},{1,9},{9,1},{17,25},{25,17},{2,10},{10... | collective-permute-start | bytes 1572872 | tf_op jit(solution)/shard_map/ppermute | solution.py:29
  117.8 19.5 %collective-permute-start.1 = (f32[256,8,4,16]{0,1,3,2:T(8,128)S(1)}, f32[256,8,4,16]{0,1,3,2:T(8,128)S(1)}, u32[]{:S(2)}, u32[]{:S(2)}) collective-permute-start(f32[256,8,4,16]{0,1,3,2:T(8,128)S(1)} %get-tuple-element.3), channel_id=1, source_target_pairs={{0,16},{8,24},{16,0},{24,8},{1,17},{9,25},{17,1},{25,9},{2,18},{10... | collective-permute-start | bytes 1572872 | tf_op jit(solution)/shard_map/ppermute | solution.py:29
  122.6 7.5 %copy-start.1 = (f32[256,8,4,16]{3,2,1,0:T(4,128)S(1)}, f32[256,8,4,16]{3,2,1,0:T(4,128)}, u32[]{:S(2)}) copy-start(f32[256,8,4,16]{3,2,1,0:T(4,128)} %copy.24) | copy-start | bytes 1572868
  122.6 27.4 %collective-permute-start.2 = (f32[256,8,4,16]{0,1,3,2:T(8,128)S(1)}, f32[256,8,4,16]{0,1,3,2:T(8,128)S(1)}, u32[]{:S(2)}, u32[]{:S(2)}) collective-permute-start(f32[256,8,4,16]{0,1,3,2:T(8,128)S(1)} %get-tuple-element.2), channel_id=1, source_target_pairs={{0,24},{8,16},{16,8},{24,0},{1,25},{9,17},{17,9},{25,1},{2,26},{10... | collective-permute-start | bytes 1572872 | tf_op jit(solution)/shard_map/ppermute | solution.py:29
  141.7 5.3 %copy-start.2 = (f32[256,8,4,16]{3,2,1,0:T(4,128)S(1)}, f32[256,8,4,16]{3,2,1,0:T(4,128)}, u32[]{:S(2)}) copy-start(f32[256,8,4,16]{3,2,1,0:T(4,128)} %copy.26) | copy-start | bytes 1572868
  174.9 6.8 %copy-start.8 = (f32[4,32]{1,0:T(4,128)S(1)}, f32[4,32]{1,0:T(4,128)}, u32[]{:S(2)}) copy-start(f32[4,32]{1,0:T(4,128)} %param.7) | copy-start | bytes 1540
  174.9 74.4 %all-to-all-start.1 = ((f32[8,1,65536]{2,1,0:T(1,128)}), f32[8,1,65536]{2,1,0:T(1,128)}, u32[]{:S(2)}, u32[]{:S(2)}) async-start(f32[8,1,65536]{2,1,0:T(1,128)} %reshape.33), calls=%async_computation.1 | async-start | bytes 4194304 | tf_op jit(solution)/shard_map/all_to_all | solution.py:34
  181.7 303.8 %all-reduce.2.cloned.1.call-start = ((), (), s32[]{:S(2)}) async-start(), calls=%async_computation.3 | async-start | bytes 8388608 | tf_op jit(solution)/shard_map/psum | solution.py:40
  346.6 158.3 %copy-start.3 = (f32[64,8,8,128]{3,1,2,0:T(8,128)S(1)}, f32[64,8,8,128]{3,1,2,0:T(8,128)}, u32[]{:S(2)}) copy-start(f32[64,8,8,128]{3,1,2,0:T(8,128)} %copy.43) | copy-start | bytes 6291460
  504.8 2.5 copy-start.5
Sparse Core Ops, SparseCore 0:
  344.9 140.6 all-reduce.1
